TPU v7x, 256 devices: a 2x2x32 block of a 4x8x32 slice. The times are simulated.
256 devices in a mesh: group: 4 (over y, x), row: 64 (over z, core).
Axes of the slice: x: 2, y: 2, z: 32, core: 2. Of those that a mesh axis runs over, the one named last changes fastest.
The devices are a block of a 4x8x32 slice.
Arguments:
- pair_repr: bfloat16 [2048, 512, 128], P(('group', 'row')), parts along dimension 0, may hold values from -60 to 60
- proj_weight: bfloat16 [128, 512], replicated, may hold values from -1.25 to 1.25
- gate_bias: float32 [128], replicated, may hold values from -4 to 4
- bias_weight: bfloat16 [128, 4], replicated, may hold values from -8 to 8
- out_weight: bfloat16 [128, 128], replicated, may hold values from -0.5 to 0.5
- out_bias: float32 [128], replicated, may hold values from -1.5 to 1.5
Outputs:
- pair_update: bfloat16 [2048, 512, 128], P(('group', 'row')), parts along dimension 0
There are 4 independent parts, one for each index of `group`. A program takes and returns all parts, laid end to end along the dimension named above; an argument that names none is the same for every part. Nothing has to cross between parts.
All inputs are finite; a program needn't handle non-finite values.
Results may differ from a plain program's by a relative error of at most 0.0085.
The roundings to bfloat16 on the way count: a program that leaves them out, or rounds other values in their place, can miss the bound.
Values may be sent and summed in bfloat16 or wider, within the bound.
A program may use at most 64 MiB of HBM per device.

v0:
```python
import math

import jax
import jax.numpy as jnp
from jax import lax
from jax.sharding import PartitionSpec as P

EPSILON = 1e-05


def normalize(pair_repr):
    values_f = pair_repr.astype(jnp.float32)
    average = jnp.mean(values_f, axis=-1, keepdims=True)
    centred = values_f - average
    variance = jnp.mean(centred * centred, axis=-1, keepdims=True)
    return (centred * lax.rsqrt(variance + EPSILON)).astype(jnp.bfloat16)


def project_heads(columns, proj_weight, gate_bias, head_count):
    projected = jnp.einsum("ncz,zf->cnf", columns, proj_weight, preferred_element_type=jnp.float32)
    inner_width = proj_weight.shape[1] // 4
    head_dim = inner_width // head_count
    head_shape = projected.shape[:2] + (head_count, head_dim)
    query = (
        (projected[..., :inner_width] * head_dim ** (-0.5)).astype(jnp.bfloat16).reshape(head_shape)
    )
    keys_all = (
        projected[..., inner_width : 2 * inner_width].astype(jnp.bfloat16).reshape(head_shape)
    )
    values = (
        projected[..., 2 * inner_width : 3 * inner_width].astype(jnp.bfloat16).reshape(head_shape)
    )
    gating = jax.nn.sigmoid(projected[..., 3 * inner_width :] + gate_bias)
    return (query, keys_all, values, gating)


def attend_block(query, keys_all, values, bias_cols):
    scores = (
        jnp.einsum("ckhd,cqhd->chkq", keys_all, query, preferred_element_type=jnp.float32)
        + bias_cols[None]
    )
    row_max = jnp.max(scores, axis=2, keepdims=True)
    expd = jnp.exp(scores - row_max)
    row_total = jnp.sum(expd, axis=2)
    attended = jnp.einsum(
        "chkq,ckhd->cqhd", expd.astype(jnp.bfloat16), values, preferred_element_type=jnp.float32
    )
    return attended / jnp.transpose(row_total, (0, 2, 1))[..., None]


def on_device(pair_repr, proj_weight, gate_bias, bias_weight, out_weight, out_bias):
    local_rows, residues, channels = pair_repr.shape
    head_count = bias_weight.shape[1]
    normed = normalize(pair_repr)
    local_bias = jnp.einsum("knc,ch->hkn", normed, bias_weight, preferred_element_type=jnp.float32)
    blocked = normed.reshape(local_rows, residues // local_rows, local_rows, channels)
    pair_bias = lax.all_gather(local_bias, "row", axis=1, tiled=True)
    query_span = min(256, residues)

    def column_group(block):
        query, keys_all, values, gating = project_heads(block, proj_weight, gate_bias, head_count)
        pieces = []
        for block_start in range(0, residues, query_span):
            pieces.append(
                attend_block(
                    query[:, block_start : block_start + query_span],
                    keys_all,
                    values,
                    pair_bias[:, :, block_start : block_start + query_span],
                )
            )
        attended = jnp.concatenate(pieces, axis=1).reshape(block.shape[1], residues, -1)
        gated = (gating * attended).astype(jnp.bfloat16)
        return jnp.transpose(gated, (1, 0, 2))

    columns = lax.all_to_all(blocked, "row", split_axis=1, concat_axis=0, tiled=True)[:, 0]
    item_count = columns.shape[1]
    group_size = math.gcd(item_count, 4)
    grouped = jnp.transpose(
        columns.reshape(residues, item_count // group_size, group_size, channels), (1, 0, 2, 3)
    )
    results = lax.map(column_group, grouped)
    results = jnp.transpose(results, (1, 0, 2, 3)).reshape(residues, item_count, -1)
    column_out = results[:, None]
    row_out = lax.all_to_all(column_out, "row", split_axis=0, concat_axis=1, tiled=True)
    row_out = row_out.reshape(local_rows, residues, -1)
    update = jnp.einsum("cnf,fz->cnz", row_out, out_weight, preferred_element_type=jnp.float32)
    return (update + out_bias).astype(jnp.bfloat16)


def solution(mesh):
    return jax.shard_map(
        on_device,
        mesh=mesh,
        in_specs=(P(("group", "row"), None, None), P(), P(), P(), P(), P()),
        out_specs=P(("group", "row"), None, None),
        check_vma=False,
    )
```

profile of v0, /device:TPU:37, one launch (start us, length us, event | category | flops | bytes accessed | tf_op | source)
XLA Modules:
  0.0 376.1 jit_solution(3074401177917555898)
XLA Ops:
  6.6 1.6 convert_reduce_fusion
  8.2 2.4 fusion.37
  10.6 2.3 fusion.38
  12.9 1.0 convolution_bitcast_fusion.1
  14.0 1.7 copy.20
  15.7 34.4 %all-to-all-start = ((bf16[8,64,8,128]{3,0,2,1:T(8,128)(2,1)}), bf16[8,64,8,128]{3,0,2,1:T(8,128)(2,1)S(1)}, u32[]{:S(2)}, u32[]{:S(2)}) async-start(bf16[8,64,8,128]{3,0,2,1:T(8,128)(2,1)} %bitcast.98), calls=%async_computation | async-start | bytes 2097152 | tf_op jit(solution)/shard_map/all_to_all | solution.py:76
  50.2 162.5 %all-gather.2.cloned.1.call-done = f32[4,512,512]{2,0,1:T(4,128)} async-done(((f32[4,8,512]{2,0,1:T(4,128)}), f32[4,512,512]{2,0,1:T(4,128)}) %all-gather.2.cloned.1.call-update) | async-done | bytes 4194320 | tf_op jit(solution)/shard_map/all_gather | solution.py:57
  212.8 5.5 %copy.23 = f32[4,512,512]{2,1,0:T(8,128)} copy(f32[4,512,512]{2,0,1:T(4,128)} %all-gather.2.cloned.1.call-done) | data formatting | bytes 8388608 | tf_op jit(solution)/shard_map/while | solution.py:82
  218.2 0.2 copy.21
  218.4 26.2 %while.10 = (s32[]{:T(128)}, bf16[2,512,4,128]{1,3,2,0:T(8,128)(2,1)}, bf16[2,512,4,128]{3,1,2,0:T(8,128)(2,1)S(1)}, bf16[128,512]{0,1:T(8,128)(2,1)S(1)}, f32[1...) while((s32[]{:T(128)}, bf16[2,512,4,128]{1,3,2,0:T(8,128)(2,1)}, bf16[2,512,4,128]{3,1,2,0:T(8,128)(2,1)S(1)}, ...), condition=%wide.region_7.8_spmd, body=%wide.region_2.7_spmd.sunk | while | flops 842514432 | bytes 107250800 | solution.py:82
  218.5 0.7 fusion.70
  219.3 0.1 fusion.73
  219.4 1.2 copy-done.1
  220.6 0.4 fusion.72
  221.0 1.4 add_reduce_fusion.5
  222.4 1.3 add_reduce_fusion.4
  223.7 3.2 fusion.74
  227.0 1.6 fusion.76
  228.6 1.6 fusion.75
  230.4 1.2 bitcast_dynamic-update-slice_fusion.2
  231.6 0.7 fusion.70
  232.5 1.3 copy-done.1
  233.7 0.4 fusion.72
  234.1 1.4 add_reduce_fusion.5
  235.5 1.3 add_reduce_fusion.4
  236.8 3.2 fusion.74
  240.1 1.6 fusion.76
  241.7 1.6 fusion.75
  243.5 1.2 bitcast_dynamic-update-slice_fusion.2
  244.7 1.7 copy.24
  246.4 121.5 %all_to_all.30 = bf16[512,1,8,128]{3,2,1,0:T(8,128)(2,1)S(1)} all-to-all(bf16[512,1,8,128]{3,2,1,0:T(8,128)(2,1)S(1)} %bitcast.99), channel_id=1, replica_groups=mesh['group'=4,'row'=64] {'row'}, dimensions={0} | all-to-all | bytes 2097152 | tf_op jit(solution)/shard_map/all_to_all | solution.py:85
  367.9 1.4 add_convert_fusion
  (24 shorter events, 0.7 us)
Async XLA Ops:
  6.5 361.3 %copy-start = (bf16[128,128]{1,0:T(8,128)(2,1)S(1)}, bf16[128,128]{1,0:T(8,128)(2,1)}, u32[]{:S(2)}) copy-start(bf16[128,128]{1,0:T(8,128)(2,1)} %param.12) | copy-start | bytes 98308
  6.6 6.3 %copy-start.4 = (bf16[128,4]{0,1:T(4,128)(2,1)S(1)}, bf16[128,4]{0,1:T(4,128)(2,1)}, u32[]{:S(2)}) copy-start(bf16[128,4]{0,1:T(4,128)(2,1)} %param.11) | copy-start | bytes 3076
  6.6 206.2 %all-gather.2.cloned.1.call-start = ((), (), s32[]{:S(2)}) async-start(), calls=%async_computation.2 | async-start | bytes 4259840 | tf_op jit(solution)/shard_map/all_gather | solution.py:57
  8.2 41.9 %copy-start.2 = (bf16[128,512]{1,0:T(8,128)(2,1)S(1)}, bf16[128,512]{1,0:T(8,128)(2,1)}, u32[]{:S(2)}) copy-start(bf16[128,512]{1,0:T(8,128)(2,1)} %param.9) | copy-start | bytes 393220
  15.7 202.5 %all-to-all-start = ((bf16[8,64,8,128]{3,0,2,1:T(8,128)(2,1)}), bf16[8,64,8,128]{3,0,2,1:T(8,128)(2,1)S(1)}, u32[]{:S(2)}, u32[]{:S(2)}) async-start(bf16[8,64,8,128]{3,0,2,1:T(8,128)(2,1)} %bitcast.98), calls=%async_computation | async-start | bytes 2097152 | tf_op jit(solution)/shard_map/all_to_all | solution.py:76
  50.2 168.2 %copy-start.3 = (f32[128]{0:T(128)S(1)}, f32[128]{0:T(128)}, u32[]{:S(2)}) copy-start(f32[128]{0:T(128)} %param.10) | copy-start | bytes 1540
  218.4 2.2 copy-start.1
  231.6 2.2 copy-start.1
  244.7 123.2 %copy-start.5 = (f32[128]{0:T(128)S(1)}, f32[128]{0:T(128)}, u32[]{:S(2)}) copy-start(f32[128]{0:T(128)} %param.13) | copy-start | bytes 1540
Sparse Core Ops, SparseCore 0:
  14.1 198.6 all-gather.1
where the time goes:
time: 379 us; the launch traced here: 376 us
  waiting for transfers between devices  163 us (43%)
  blocking collectives  121 us (32%)
  starting transfers between devices  34.4 us (9%)
  matrix products  15.8 us (4%)
  other arithmetic  15.6 us (4%)
  between operations  13.5 us (4%)
  local copies, waits for them, and re-layouts  12.6 us (3%)
    all_gather x1, waiting for transfers between devices, on_device(): pair_bias = lax.all_gather(local_bias, 'row', axis=1, tiled=True)  163 us
    all_to_all x1, blocking collectives, on_device(): lax.all_to_all(column_out, 'row', split_axis=0, concat_axis=1, tiled=True)  121 us
    all_to_all x1, starting transfers between devices, on_device(): lax.all_to_all(blocked, 'row', split_axis=1, concat_axis=0, tiled=True)  34.4 us
  transfers between devices with their start and end apart: 2, of which 1 were waited for; matrix products, arithmetic and copies ran while one was open for 2% of the time, Pallas kernels for 0%

commit v1 on v0

v1 whole, which is shorter than its diff:
```python
import functools

import jax
import jax.numpy as jnp
from jax import lax
from jax.experimental import pallas as pl
from jax.experimental.pallas import tpu as pltpu
from jax.sharding import PartitionSpec as P

EPSILON = 1e-05
MESH = pl.DeviceIdType.MESH
LANES = 128
NT = (((1,), (1,)), ((), ()))


def nt_dot(a, b):
    return lax.dot_general(a, b, NT, preferred_element_type=jnp.float32)


def exchange_kernel(
    chips,
    heads,
    x_ref,
    proj_ref,
    gate_bias_ref,
    bias_weight_ref,
    out_ref,
    xin,
    flat,
    bias_rows,
    send_buf,
    cols,
    bias,
    proj_t,
    gate_col,
    keys,
    values_t,
    result,
    send_out,
    in_local_sem,
    in_send_sem,
    in_recv_sem,
    ring_send_sem,
    ring_recv_sem,
    pair_send_sem,
    pair_recv_sem,
    a2a_send_sem,
    a2a_recv_sem,
    out_local_sem,
    out_send_sem,
    out_recv_sem,
):
    local_rows = x_ref.shape[0]
    pair_rows = 2 * local_rows
    blocks = cols.shape[2]
    spread = cols.shape[1]
    width = cols.shape[0]
    channels = x_ref.shape[4]
    half = send_buf.shape[0] * width
    row = lax.axis_index("row")
    chip = row // 2
    core = lax.rem(row, 2)
    partner = row + 1 - 2 * core
    last = chips // 2

    def at(distance):
        return lax.rem(row + 2 * distance + 2 * chips, 2 * chips)

    barrier = pltpu.get_barrier_semaphore()
    for other in (partner, at(1), at(-1)):
        pl.semaphore_signal(barrier, inc=1, device_id={"row": other}, device_id_type=MESH)

    proj_t[...] = proj_ref[...].astype(jnp.float32).T.astype(jnp.bfloat16)
    gate_col[...] = jnp.broadcast_to(gate_bias_ref[...], (channels, channels)).T
    eye = (
        lax.broadcasted_iota(jnp.int32, (8, heads), 0) == lax.broadcasted_iota(jnp.int32, (8, heads), 1)
    ).astype(jnp.float32)
    bias_w = nt_dot(eye, bias_weight_ref[...].astype(jnp.float32)).astype(jnp.bfloat16)

    keep = pltpu.make_async_copy(x_ref.at[:, :, core], xin.at[core], in_local_sem)
    keep.start()
    pl.semaphore_wait(barrier, 3)
    swap = pltpu.make_async_remote_copy(
        src_ref=x_ref.at[:, :, 1 - core],
        dst_ref=xin.at[core],
        send_sem=in_send_sem,
        recv_sem=in_recv_sem,
        device_id={"row": partner},
        device_id_type=MESH,
    )
    swap.start()
    keep.wait()
    swap.wait()

    def normalize_row(index, _):
        part = index // local_rows
        line = lax.rem(index, local_rows)
        x = xin[part, line].reshape(half, channels).astype(jnp.float32)
        centred = x - jnp.mean(x, axis=-1, keepdims=True)
        variance = jnp.mean(centred * centred, axis=-1, keepdims=True)
        normed = centred * lax.rsqrt(variance + EPSILON)
        rounded = normed.astype(jnp.bfloat16)
        groups = [rounded[g * pair_rows : (g + 1) * pair_rows] for g in range(half // pair_rows)]
        ordered = [groups[a * (blocks // 2) + block] for block in range(blocks // 2) for a in range(spread)]
        row_bias = nt_dot(bias_w, jnp.concatenate(ordered, axis=0))
        for block in range(blocks // 2):
            lanes = slice(block * LANES, (block + 1) * LANES)
            bias_rows[block, pl.ds(pl.multiple_of(index * 8, 8), 8), :] = row_bias[:, lanes]
        flat[pl.ds(index, half, stride=pair_rows), :] = normed
        return 0

    lax.fori_loop(0, pair_rows, normalize_row, 0)
    for block in range(blocks // 2):
        for h in range(heads):
            piece = bias_rows[block, pl.ds(h, pair_rows, stride=8), :]
            bias[core * (blocks // 2) + block, chip, :, h * LANES : (h + 1) * LANES] = piece

    mine = pl.ds(core * (blocks // 2), blocks // 2)

    def ring_copy(source, step, direction, target):
        ref = bias.at[mine, source]
        return pltpu.make_async_remote_copy(
            src_ref=ref,
            dst_ref=ref,
            send_sem=ring_send_sem,
            recv_sem=ring_recv_sem.at[direction, step],
            device_id={"row": target},
            device_id_type=MESH,
        )

    def pair_copy(source):
        ref = bias.at[mine, source]
        return pltpu.make_async_remote_copy(
            src_ref=ref,
            dst_ref=ref,
            send_sem=pair_send_sem,
            recv_sem=pair_recv_sem,
            device_id={"row": partner},
            device_id_type=MESH,
        )

    def column_copy(distance):
        target = at(distance)
        target_chip = target // 2
        return pltpu.make_async_remote_copy(
            src_ref=send_buf.at[target_chip],
            dst_ref=cols.at[:, chip // blocks, lax.rem(chip, blocks)],
            send_sem=a2a_send_sem,
            recv_sem=a2a_recv_sem,
            device_id={"row": target},
            device_id_type=MESH,
        )

    ring_copy(chip, 0, 0, at(1)).start()
    ring_copy(chip, 0, 1, at(-1)).start()
    pair_copy(chip).start()

    def round_chunk(index, _):
        rows = width * pair_rows
        piece = flat[pl.ds(pl.multiple_of(index * rows, rows), rows), :]
        send_buf[index] = piece.reshape(width, pair_rows, channels).astype(jnp.bfloat16)
        return 0

    lax.fori_loop(0, chips, round_chunk, 0)
    cols[:, chip // blocks, lax.rem(chip, blocks)] = send_buf[chip]

    def chip_at(distance):
        return at(distance) // 2

    def ring_step(step, _):
        behind, ahead = chip_at(-step), chip_at(step)
        ring_copy(behind, step - 1, 0, at(1)).wait_recv()
        ring_copy(behind, step, 0, at(1)).start()
        ring_copy(ahead, step - 1, 1, at(-1)).wait_recv()

        @pl.when(step < last - 1)
        def _():
            ring_copy(ahead, step, 1, at(-1)).start()

        pair_copy(behind).start()
        pair_copy(ahead).start()
        column_copy(step).start()
        column_copy(-step).start()
        return 0

    lax.fori_loop(1, last, ring_step, 0)
    opposite = chip_at(-last)
    ring_copy(opposite, last - 1, 0, at(1)).wait_recv()
    pair_copy(opposite).start()
    column_copy(last).start()

    whole = bias.at[mine]
    pltpu.make_async_copy(whole, whole, pair_recv_sem).wait()
    others = send_buf.at[pl.ds(0, chips - 1)]
    pltpu.make_async_copy(others, others, a2a_recv_sem).wait()

    inner = proj_t.shape[0] // 4
    head_dim = inner // heads
    residues = chips * pair_rows
    block_rows = spread * pair_rows

    def project(column, _):
        x = cols[column].reshape(residues, channels)
        keys[column] = nt_dot(x, proj_t[inner : 2 * inner]).astype(jnp.bfloat16)
        values_t[column] = nt_dot(proj_t[2 * inner : 3 * inner], x).astype(jnp.bfloat16)
        return 0

    lax.fori_loop(0, width, project, 0)

    head_of_row = lax.broadcasted_iota(jnp.int32, (inner, block_rows), 0) // head_dim
    group = (chip // blocks) * (2 * blocks) + core * blocks + lax.rem(chip, blocks)

    def attend(column, block):
        x = cols[column, :, block].reshape(block_rows, channels)
        query_t = nt_dot(proj_t[0:inner], x) * head_dim ** (-0.5)
        gate_t = jax.nn.sigmoid(nt_dot(proj_t[3 * inner : 4 * inner], x) + gate_col[...])
        spread_q = jnp.concatenate(
            [jnp.where(head_of_row == h, query_t, 0.0).astype(jnp.bfloat16) for h in range(heads)], axis=1
        )
        scores = jnp.dot(keys[column], spread_q, preferred_element_type=jnp.float32)
        scores = scores + bias[block].reshape(residues, heads * block_rows)
        row_max = jnp.max(scores, axis=0, keepdims=True)
        expd = jnp.exp(scores - row_max)
        row_total = jnp.sum(expd, axis=0, keepdims=True)
        summed = jnp.dot(values_t[column], expd.astype(jnp.bfloat16), preferred_element_type=jnp.float32)
        parts = []
        for h in range(heads):
            lanes = slice(h * block_rows, (h + 1) * block_rows)
            parts.append(summed[h * head_dim : (h + 1) * head_dim, lanes] / row_total[:, lanes])
        gated_t = gate_t * jnp.concatenate(parts, axis=0)
        result[pl.ds(column, block_rows, stride=width), :] = gated_t.T

    def out_copy(block, a, target_core):
        target_chip = a * blocks + block
        return pltpu.make_async_remote_copy(
            src_ref=send_out.at[block, a, target_core],
            dst_ref=out_ref.at[:, group],
            send_sem=out_send_sem,
            recv_sem=out_recv_sem,
            device_id={"row": 2 * target_chip + target_core},
            device_id_type=MESH,
        )

    def block_step(step, _):
        block = lax.rem(chip + step, blocks)

        def column_step(column, _):
            attend(column, block)
            return 0

        lax.fori_loop(0, width, column_step, 0)
        send_out[block] = (
            result[...].reshape(spread, 2, local_rows, width, channels).astype(jnp.bfloat16)
        )

        def send(index, _):
            a = index // 2
            target_core = lax.rem(index, 2)
            own = 2 * (a * blocks + block) + target_core == row

            @pl.when(jnp.logical_not(own))
            def _():
                out_copy(block, a, target_core).start()

            return 0

        lax.fori_loop(0, 2 * spread, send, 0)
        return 0

    lax.fori_loop(0, blocks, block_step, 0)
    own_copy = pltpu.make_async_copy(
        send_out.at[lax.rem(chip, blocks), chip // blocks, core], out_ref.at[:, group], out_local_sem
    )
    own_copy.start()

    ring_blocks = bias.at[mine, pl.ds(0, chips - 1)]
    pltpu.make_async_copy(ring_blocks, ring_blocks, ring_send_sem).wait()
    pltpu.make_async_copy(whole, whole, pair_send_sem).wait()
    pltpu.make_async_copy(others, others, a2a_send_sem).wait()
    own_copy.wait()
    received = out_ref.at[:, pl.ds(0, 2 * chips - 1)]
    pltpu.make_async_copy(received, received, out_send_sem).wait()
    pltpu.make_async_copy(received, received, out_recv_sem).wait()


def on_device(row_count, pair_repr, proj_weight, gate_bias, bias_weight, out_weight, out_bias):
    local_rows, residues, channels = pair_repr.shape
    heads = bias_weight.shape[1]
    inner = proj_weight.shape[1] // 4
    chips = row_count // 2
    width = residues // row_count
    pair_rows = 2 * local_rows
    blocks = residues // LANES
    spread = chips // blocks
    vmem = pl.BlockSpec(memory_space=pltpu.VMEM)
    dma = pltpu.SemaphoreType.DMA
    gathered = pl.pallas_call(
        functools.partial(exchange_kernel, chips, heads),
        out_shape=jax.ShapeDtypeStruct((local_rows, row_count, width, channels), jnp.bfloat16),
        in_specs=[pl.BlockSpec(memory_space=pl.ANY), vmem, vmem, vmem],
        out_specs=pl.BlockSpec(memory_space=pl.ANY),
        scratch_shapes=[
            pltpu.VMEM((2, local_rows, spread, residues // (2 * spread), channels), jnp.bfloat16),
            pltpu.VMEM((residues // 2 * pair_rows, channels), jnp.float32),
            pltpu.VMEM((blocks // 2, 8 * pair_rows, LANES), jnp.float32),
            pltpu.VMEM((chips, width, pair_rows, channels), jnp.bfloat16),
            pltpu.VMEM((width, spread, blocks, pair_rows, channels), jnp.bfloat16),
            pltpu.VMEM((blocks, chips, pair_rows, heads * LANES), jnp.float32),
            pltpu.VMEM((4 * inner, channels), jnp.bfloat16),
            pltpu.VMEM((channels, channels), jnp.float32),
            pltpu.VMEM((width, residues, inner), jnp.bfloat16),
            pltpu.VMEM((width, inner, residues), jnp.bfloat16),
            pltpu.VMEM((LANES * width, inner), jnp.float32),
            pltpu.VMEM((blocks, spread, 2, local_rows, width, inner), jnp.bfloat16),
            dma,
            dma,
            dma,
            dma,
            dma((2, chips // 2)),
            dma,
            dma,
            dma,
            dma,
            dma,
            dma,
            dma,
        ],
        compiler_params=pltpu.CompilerParams(collective_id=0, has_side_effects=True, vmem_limit_bytes=60 * 2**20),
    )(
        pair_repr.reshape(local_rows, spread, 2, residues // (2 * spread), channels),
        proj_weight,
        gate_bias.reshape(1, inner),
        bias_weight,
    )
    gated = gathered.reshape(local_rows, residues, inner)
    update = jnp.einsum("cnf,fz->cnz", gated, out_weight, preferred_element_type=jnp.float32)
    return (update + out_bias).astype(jnp.bfloat16)


def solution(mesh):
    return jax.shard_map(
        functools.partial(on_device, mesh.shape["row"]),
        mesh=mesh,
        in_specs=(P(("group", "row"), None, None), P(), P(), P(), P(), P()),
        out_specs=P(("group", "row"), None, None),
        check_vma=False,
    )
```

time: 379 us -> 259 us (0.68)
  Pallas kernels: 0 us -> 254 us
  waiting for transfers between devices: 163 us -> 0 us
  blocking collectives: 121 us -> 0 us
  starting transfers between devices: 34.4 us -> 0 us
  other arithmetic: 15.6 us -> 0 us
  between operations: 13.5 us -> 0.03 us
  matrix products: 15.8 us -> 2.62 us
  local copies, waits for them, and re-layouts: 12.6 us -> 1.42 us
    pallas_call x0 -> x1, Pallas kernels: none -> 254 us  [on_device(): pl.pallas_call(functools.partial(exchange_kernel, chips, heads), out_shap...]
    all_gather x1 -> x0, waiting for transfers between devices: 163 us -> none  [on_device(): pair_bias = lax.all_gather(local_bias, 'row', axis=1, tiled=True)]
    all_to_all x1 -> x0, blocking collectives: 121 us -> none  [on_device(): lax.all_to_all(column_out, 'row', split_axis=0, concat_axis=1, tiled=True)]
    all_to_all x1 -> x0, starting transfers between devices: 34.4 us -> none  [on_device(): lax.all_to_all(blocked, 'row', split_axis=1, concat_axis=0, tiled=True)]
    dot_general x12 -> x1, matrix products: 15.8 us -> 2.62 us  [on_device(): jnp.einsum('cnf,fz->cnz', gated, out_weight, preferred_element_type=jnp.f...]
    reduce_sum x4 -> x0, other arithmetic: 10.5 us -> none  [the longest x2 6.5 us: attend_block(): row_total = jnp.sum(expd, axis=2)]
    while x6 -> x0, local copies, waits for them, and re-layouts: 8.1 us -> none  [the longest x2 5.6 us: on_device(): results = lax.map(column_group, grouped)]
  transfers between devices with their start and end apart: 2 -> 0, of which waited for: 1 -> 0; matrix products, arithmetic and copies ran while one was open for 2% -> 0% of each run, Pallas kernels for 0% -> 0%
where the time goes in v1:
time: 259 us; the launch traced here: 258 us
  Pallas kernels  254 us (98%)
  matrix products  2.62 us (1%)
    pallas_call x1, Pallas kernels, on_device(): pl.pallas_call(functools.partial(exchange_kernel, chips, heads), out_shap...  254 us

profile of v1, /device:TPU:37, one launch (start us, length us, event | category | flops | bytes accessed | tf_op | source)
XLA Modules:
  0.0 258.3 jit_solution(10724689394849698459)
XLA Ops:
  0.0 0.0 copy-start
  0.0 1.4 copy.7.bias_weight_ref
  1.4 0.0 copy-start.1
  1.4 254.3 %shard_map.64 = bf16[8,64,8,128]{3,2,1,0:T(8,128)(2,1)} custom-call(bf16[8,8,2,32,128]{4,3,2,1,0:T(8,128)(2,1)} %bitcast.8, bf16[128,512]{1,0:T(8,128)(2,1)} %proj_ref.1, f32[1,128]{1,0:T(1,128)} %bitcast.9, bf16[128,4]{1,0:T(8,128)(2,1)} %copy.7.bias_weight_ref), custom_call_target="tpu_custom_call" | custom-call | tf_op jit(solution)/shard_map/pallas_call | solution.py:297
  255.7 0.0 copy-done
  255.7 0.0 copy-done.1
  255.7 2.6 %add_convert_fusion = bf16[8,512,128]{2,1,0:T(8,128)(2,1)} fusion(bf16[8,64,8,128]{3,2,1,0:T(8,128)(2,1)} %shard_map.64, f32[128]{0:T(128)S(1)} %copy-done.1, bf16[128,128]{1,0:T(8,128)(2,1)S(1)} %copy-done), kind=kOutput, calls=%fused_computation | convolution fusion | flops 135266304 | bytes 2130432 | tf_op jit(solution)/shard_map/cnf,fz->cnz/dot_general | solution.py:336
Async XLA Ops:
  0.0 255.7 %copy-start = (bf16[128,128]{1,0:T(8,128)(2,1)S(1)}, bf16[128,128]{1,0:T(8,128)(2,1)}, u32[]{:S(2)}) copy-start(bf16[128,128]{1,0:T(8,128)(2,1)} %param.10) | copy-start | bytes 98308
  1.4 254.3 %copy-start.1 = (f32[128]{0:T(128)S(1)}, f32[128]{0:T(128)}, u32[]{:S(2)}) copy-start(f32[128]{0:T(128)} %param.11) | copy-start | bytes 1540

commit v2 on v1

--- a/solution.py
+++ b/solution.py
@@ -21,10 +21,13 @@
     chips,
     heads,
     x_ref,
+    proj_hbm,
+    gate_bias_hbm,
+    bias_weight_hbm,
+    out_ref,
     proj_ref,
     gate_bias_ref,
     bias_weight_ref,
-    out_ref,
     xin,
     flat,
     bias_rows,
@@ -37,6 +40,7 @@
     values_t,
     result,
     send_out,
+    weight_sems,
     in_local_sem,
     in_send_sem,
     in_recv_sem,
@@ -46,7 +50,6 @@
     pair_recv_sem,
     a2a_send_sem,
     a2a_recv_sem,
-    out_local_sem,
     out_send_sem,
     out_recv_sem,
 ):
@@ -62,6 +65,8 @@
     core = lax.rem(row, 2)
     partner = row + 1 - 2 * core
     last = chips // 2
+    first, tail = width // 2, width // 8
+    chunks = ((0, first), (first, width - first - tail), (width - tail, tail))
 
     def at(distance):
         return lax.rem(row + 2 * distance + 2 * chips, 2 * chips)
@@ -69,16 +74,24 @@
     barrier = pltpu.get_barrier_semaphore()
     for other in (partner, at(1), at(-1)):
         pl.semaphore_signal(barrier, inc=1, device_id={"row": other}, device_id_type=MESH)
+    keep = pltpu.make_async_copy(x_ref.at[:, :, core], xin.at[core], in_local_sem)
+    keep.start()
+    weight_copies = [
+        pltpu.make_async_copy(source, target, weight_sems.at[i])
+        for i, (source, target) in enumerate(
+            ((proj_hbm, proj_ref), (gate_bias_hbm, gate_bias_ref), (bias_weight_hbm, bias_weight_ref))
+        )
+    ]
+    for copy in weight_copies:
+        copy.start()
+    for copy in weight_copies:
+        copy.wait()
 
     proj_t[...] = proj_ref[...].astype(jnp.float32).T.astype(jnp.bfloat16)
     gate_col[...] = jnp.broadcast_to(gate_bias_ref[...], (channels, channels)).T
-    eye = (
-        lax.broadcasted_iota(jnp.int32, (8, heads), 0) == lax.broadcasted_iota(jnp.int32, (8, heads), 1)
-    ).astype(jnp.float32)
-    bias_w = nt_dot(eye, bias_weight_ref[...].astype(jnp.float32)).astype(jnp.bfloat16)
-
-    keep = pltpu.make_async_copy(x_ref.at[:, :, core], xin.at[core], in_local_sem)
-    keep.start()
+    bias_w = bias_weight_ref[...].astype(jnp.float32)
+    bias_w = jnp.concatenate([bias_w, jnp.zeros((8 - heads, channels), jnp.float32)], axis=0).astype(jnp.bfloat16)
+
     pl.semaphore_wait(barrier, 3)
     swap = pltpu.make_async_remote_copy(
         src_ref=x_ref.at[:, :, 1 - core],
@@ -90,11 +103,9 @@
     )
     swap.start()
     keep.wait()
-    swap.wait()
-
-    def normalize_row(index, _):
-        part = index // local_rows
-        line = lax.rem(index, local_rows)
+
+    def normalize_row(part, line):
+        index = part * local_rows + line
         x = xin[part, line].reshape(half, channels).astype(jnp.float32)
         centred = x - jnp.mean(x, axis=-1, keepdims=True)
         variance = jnp.mean(centred * centred, axis=-1, keepdims=True)
@@ -107,9 +118,18 @@
             lanes = slice(block * LANES, (block + 1) * LANES)
             bias_rows[block, pl.ds(pl.multiple_of(index * 8, 8), 8), :] = row_bias[:, lanes]
         flat[pl.ds(index, half, stride=pair_rows), :] = normed
-        return 0
-
-    lax.fori_loop(0, pair_rows, normalize_row, 0)
+
+    def own_row(line, _):
+        normalize_row(core, line)
+        return 0
+
+    def other_row(line, _):
+        normalize_row(1 - core, line)
+        return 0
+
+    lax.fori_loop(0, local_rows, own_row, 0)
+    swap.wait()
+    lax.fori_loop(0, local_rows, other_row, 0)
     for block in range(blocks // 2):
         for h in range(heads):
             piece = bias_rows[block, pl.ds(h, pair_rows, stride=8), :]
@@ -139,14 +159,14 @@
             device_id_type=MESH,
         )
 
-    def column_copy(distance):
+    def column_copy(distance, chunk):
         target = at(distance)
-        target_chip = target // 2
+        part = pl.ds(*chunks[chunk])
         return pltpu.make_async_remote_copy(
-            src_ref=send_buf.at[target_chip],
-            dst_ref=cols.at[:, chip // blocks, lax.rem(chip, blocks)],
+            src_ref=send_buf.at[target // 2, part],
+            dst_ref=cols.at[part, chip // blocks, lax.rem(chip, blocks)],
             send_sem=a2a_send_sem,
-            recv_sem=a2a_recv_sem,
+            recv_sem=a2a_recv_sem.at[chunk],
             device_id={"row": target},
             device_id_type=MESH,
         )
@@ -179,20 +199,27 @@
 
         pair_copy(behind).start()
         pair_copy(ahead).start()
-        column_copy(step).start()
-        column_copy(-step).start()
+        column_copy(step, 0).start()
+        column_copy(-step, 0).start()
         return 0
 
     lax.fori_loop(1, last, ring_step, 0)
     opposite = chip_at(-last)
     ring_copy(opposite, last - 1, 0, at(1)).wait_recv()
     pair_copy(opposite).start()
-    column_copy(last).start()
+    column_copy(last, 0).start()
+    for chunk in range(1, len(chunks)):
+        column_copy(last, chunk).start()
+
+        def send_columns(nearer, _, chunk=chunk):
+            column_copy(last - nearer, chunk).start()
+            column_copy(nearer - last, chunk).start()
+            return 0
+
+        lax.fori_loop(1, last, send_columns, 0)
 
     whole = bias.at[mine]
-    pltpu.make_async_copy(whole, whole, pair_recv_sem).wait()
     others = send_buf.at[pl.ds(0, chips - 1)]
-    pltpu.make_async_copy(others, others, a2a_recv_sem).wait()
 
     inner = proj_t.shape[0] // 4
     head_dim = inner // heads
@@ -204,8 +231,6 @@
         keys[column] = nt_dot(x, proj_t[inner : 2 * inner]).astype(jnp.bfloat16)
         values_t[column] = nt_dot(proj_t[2 * inner : 3 * inner], x).astype(jnp.bfloat16)
         return 0
-
-    lax.fori_loop(0, width, project, 0)
 
     head_of_row = lax.broadcasted_iota(jnp.int32, (inner, block_rows), 0) // head_dim
     group = (chip // blocks) * (2 * blocks) + core * blocks + lax.rem(chip, blocks)
@@ -228,7 +253,7 @@
             lanes = slice(h * block_rows, (h + 1) * block_rows)
             parts.append(summed[h * head_dim : (h + 1) * head_dim, lanes] / row_total[:, lanes])
         gated_t = gate_t * jnp.concatenate(parts, axis=0)
-        result[pl.ds(column, block_rows, stride=width), :] = gated_t.T
+        result[block, pl.ds(column, block_rows, stride=width), :] = gated_t.T
 
     def out_copy(block, a, target_core):
         target_chip = a * blocks + block
@@ -241,43 +266,55 @@
             device_id_type=MESH,
         )
 
-    def block_step(step, _):
+    def attend_block(step, chunk):
         block = lax.rem(chip + step, blocks)
+        start, count = chunks[chunk]
 
         def column_step(column, _):
             attend(column, block)
             return 0
 
-        lax.fori_loop(0, width, column_step, 0)
-        send_out[block] = (
-            result[...].reshape(spread, 2, local_rows, width, channels).astype(jnp.bfloat16)
-        )
+        lax.fori_loop(start, start + count, column_step, 0)
+        return block
+
+    def send_block(step, _):
+        block = attend_block(step, len(chunks) - 1)
+        send_out[block] = result[block].reshape(spread, 2, local_rows, width, channels).astype(jnp.bfloat16)
 
         def send(index, _):
-            a = index // 2
-            target_core = lax.rem(index, 2)
-            own = 2 * (a * blocks + block) + target_core == row
-
-            @pl.when(jnp.logical_not(own))
+            order = index // 2
+            jump = spread // 2 + (order // 2 + lax.rem(order, 2)) * (1 - 2 * lax.rem(order, 2))
+            target_chip = lax.rem(chip + step + blocks * jump, chips)
+            target_core = lax.rem(core + index, 2)
+
+            @pl.when(2 * target_chip + target_core != row)
             def _():
-                out_copy(block, a, target_core).start()
+                out_copy(block, target_chip // blocks, target_core).start()
 
             return 0
 
         lax.fori_loop(0, 2 * spread, send, 0)
         return 0
 
-    lax.fori_loop(0, blocks, block_step, 0)
-    own_copy = pltpu.make_async_copy(
-        send_out.at[lax.rem(chip, blocks), chip // blocks, core], out_ref.at[:, group], out_local_sem
-    )
-    own_copy.start()
+    pltpu.make_async_copy(whole, whole, pair_recv_sem).wait()
+    for chunk, (start, count) in enumerate(chunks):
+        arrived = send_buf.at[pl.ds(0, chips - 1), pl.ds(0, count)]
+        pltpu.make_async_copy(arrived, arrived, a2a_recv_sem.at[chunk]).wait()
+        lax.fori_loop(start, start + count, project, 0)
+        if chunk < len(chunks) - 1:
+
+            def attend_early(step, _, chunk=chunk):
+                attend_block(step, chunk)
+                return 0
+
+            lax.fori_loop(0, blocks, attend_early, 0)
+    lax.fori_loop(0, blocks, send_block, 0)
+    out_ref[:, group] = send_out[lax.rem(chip, blocks), chip // blocks, core]
 
     ring_blocks = bias.at[mine, pl.ds(0, chips - 1)]
     pltpu.make_async_copy(ring_blocks, ring_blocks, ring_send_sem).wait()
     pltpu.make_async_copy(whole, whole, pair_send_sem).wait()
     pltpu.make_async_copy(others, others, a2a_send_sem).wait()
-    own_copy.wait()
     received = out_ref.at[:, pl.ds(0, 2 * chips - 1)]
     pltpu.make_async_copy(received, received, out_send_sem).wait()
     pltpu.make_async_copy(received, received, out_recv_sem).wait()
@@ -292,14 +329,16 @@
     pair_rows = 2 * local_rows
     blocks = residues // LANES
     spread = chips // blocks
-    vmem = pl.BlockSpec(memory_space=pltpu.VMEM)
     dma = pltpu.SemaphoreType.DMA
     gathered = pl.pallas_call(
         functools.partial(exchange_kernel, chips, heads),
         out_shape=jax.ShapeDtypeStruct((local_rows, row_count, width, channels), jnp.bfloat16),
-        in_specs=[pl.BlockSpec(memory_space=pl.ANY), vmem, vmem, vmem],
-        out_specs=pl.BlockSpec(memory_space=pl.ANY),
+        in_specs=[pl.BlockSpec(memory_space=pltpu.HBM)] * 4,
+        out_specs=pl.BlockSpec(memory_space=pltpu.VMEM),
         scratch_shapes=[
+            pltpu.VMEM((channels, 4 * inner), jnp.bfloat16),
+            pltpu.VMEM((1, inner), jnp.float32),
+            pltpu.VMEM((heads, channels), jnp.bfloat16),
             pltpu.VMEM((2, local_rows, spread, residues // (2 * spread), channels), jnp.bfloat16),
             pltpu.VMEM((residues // 2 * pair_rows, channels), jnp.float32),
             pltpu.VMEM((blocks // 2, 8 * pair_rows, LANES), jnp.float32),
@@ -310,8 +349,9 @@
             pltpu.VMEM((channels, channels), jnp.float32),
             pltpu.VMEM((width, residues, inner), jnp.bfloat16),
             pltpu.VMEM((width, inner, residues), jnp.bfloat16),
-            pltpu.VMEM((LANES * width, inner), jnp.float32),
+            pltpu.VMEM((blocks, LANES * width, inner), jnp.float32),
             pltpu.VMEM((blocks, spread, 2, local_rows, width, inner), jnp.bfloat16),
+            dma((3,)),
             dma,
             dma,
             dma,
@@ -320,17 +360,21 @@
             dma,
             dma,
             dma,
-            dma,
-            dma,
+            dma((3,)),
             dma,
             dma,
         ],
-        compiler_params=pltpu.CompilerParams(collective_id=0, has_side_effects=True, vmem_limit_bytes=60 * 2**20),
+        compiler_params=pltpu.CompilerParams(collective_id=0, has_side_effects=True, vmem_limit_bytes=28 * 2**20),
     )(
-        pair_repr.reshape(local_rows, spread, 2, residues // (2 * spread), channels),
-        proj_weight,
-        gate_bias.reshape(1, inner),
-        bias_weight,
+        *(
+            pltpu.with_memory_space_constraint(array, pltpu.HBM)
+            for array in (
+                pair_repr.reshape(local_rows, spread, 2, residues // (2 * spread), channels),
+                proj_weight,
+                gate_bias.reshape(1, inner),
+                bias_weight.T,
+            )
+        )
     )
     gated = gathered.reshape(local_rows, residues, inner)
     update = jnp.einsum("cnf,fz->cnz", gated, out_weight, preferred_element_type=jnp.float32)

time: 259 us -> 250 us (0.965)
  Pallas kernels: 254 us -> 248 us
    pallas_call x1, Pallas kernels: 254 us -> 248 us  [on_device(): pl.pallas_call(functools.partial(exchange_kernel, chips, heads), out_shap...]
where the time goes in v2:
time: 250 us
  Pallas kernels  248 us (99%)
    pallas_call x1, Pallas kernels, on_device(): pl.pallas_call(functools.partial(exchange_kernel, chips, heads), out_shap...  248 us

profile of v2, /device:TPU:37, one launch (start us, length us, event | category | flops | bytes accessed | tf_op | source)
XLA Modules:
  0.0 249.9 jit_solution(17640391992442661410)
XLA Ops:
  0.0 0.0 copy-start
  0.0 0.0 copy-start.1
  0.0 248.4 %shard_map.64 = bf16[8,64,8,128]{3,2,1,0:T(8,128)(2,1)S(1)} custom-call(bf16[8,8,2,32,128]{4,3,2,1,0:T(8,128)(2,1)} %bitcast.9, bf16[128,512]{1,0:T(8,128)(2,1)} %proj_hbm.1, f32[1,128]{1,0:T(1,128)} %bitcast.11, bf16[4,128]{1,0:T(4,128)(2,1)} %bitcast.10), custom_call_target="tpu_custom_call" | custom-call | tf_op jit(solution)/shard_map/pallas_call | solution.py:333
  248.5 0.0 copy-done
  248.5 0.0 copy-done.1
  248.5 1.4 add_convert_fusion
Async XLA Ops:
  0.0 248.5 %copy-start = (bf16[128,128]{1,0:T(8,128)(2,1)S(1)}, bf16[128,128]{1,0:T(8,128)(2,1)}, u32[]{:S(2)}) copy-start(bf16[128,128]{1,0:T(8,128)(2,1)} %param.10) | copy-start | bytes 98308
  0.0 248.5 %copy-start.1 = (f32[128]{0:T(128)S(1)}, f32[128]{0:T(128)}, u32[]{:S(2)}) copy-start(f32[128]{0:T(128)} %param.11) | copy-start | bytes 1540

commit v3 on v2

--- a/solution.py
+++ b/solution.py
@@ -38,7 +38,6 @@
     gate_col,
     keys,
     values_t,
-    result,
     send_out,
     weight_sems,
     in_local_sem,
@@ -65,8 +64,8 @@
     core = lax.rem(row, 2)
     partner = row + 1 - 2 * core
     last = chips // 2
-    first, tail = width // 2, width // 8
-    chunks = ((0, first), (first, width - first - tail), (width - tail, tail))
+    first = width // 2
+    chunks = ((0, first), (first, width - first))
 
     def at(distance):
         return lax.rem(row + 2 * distance + 2 * chips, 2 * chips)
@@ -253,20 +252,21 @@
             lanes = slice(h * block_rows, (h + 1) * block_rows)
             parts.append(summed[h * head_dim : (h + 1) * head_dim, lanes] / row_total[:, lanes])
         gated_t = gate_t * jnp.concatenate(parts, axis=0)
-        result[block, pl.ds(column, block_rows, stride=width), :] = gated_t.T
-
-    def out_copy(block, a, target_core):
-        target_chip = a * blocks + block
+        rows = gated_t.T.reshape(spread, 2, local_rows, channels)
+        send_out[block, :, :, column] = rows.astype(jnp.bfloat16)
+
+    def out_copy(block, a, target_core, chunk):
+        part = pl.ds(*chunks[chunk])
         return pltpu.make_async_remote_copy(
-            src_ref=send_out.at[block, a, target_core],
-            dst_ref=out_ref.at[:, group],
+            src_ref=send_out.at[block, a, target_core, part],
+            dst_ref=out_ref.at[group, part],
             send_sem=out_send_sem,
             recv_sem=out_recv_sem,
-            device_id={"row": 2 * target_chip + target_core},
+            device_id={"row": 2 * (a * blocks + block) + target_core},
             device_id_type=MESH,
         )
 
-    def attend_block(step, chunk):
+    def block_step(step, chunk):
         block = lax.rem(chip + step, blocks)
         start, count = chunks[chunk]
 
@@ -275,11 +275,6 @@
             return 0
 
         lax.fori_loop(start, start + count, column_step, 0)
-        return block
-
-    def send_block(step, _):
-        block = attend_block(step, len(chunks) - 1)
-        send_out[block] = result[block].reshape(spread, 2, local_rows, width, channels).astype(jnp.bfloat16)
 
         def send(index, _):
             order = index // 2
@@ -289,33 +284,30 @@
 
             @pl.when(2 * target_chip + target_core != row)
             def _():
-                out_copy(block, target_chip // blocks, target_core).start()
+                out_copy(block, target_chip // blocks, target_core, chunk).start()
 
             return 0
 
         lax.fori_loop(0, 2 * spread, send, 0)
-        return 0
 
     pltpu.make_async_copy(whole, whole, pair_recv_sem).wait()
     for chunk, (start, count) in enumerate(chunks):
         arrived = send_buf.at[pl.ds(0, chips - 1), pl.ds(0, count)]
         pltpu.make_async_copy(arrived, arrived, a2a_recv_sem.at[chunk]).wait()
         lax.fori_loop(start, start + count, project, 0)
-        if chunk < len(chunks) - 1:
-
-            def attend_early(step, _, chunk=chunk):
-                attend_block(step, chunk)
-                return 0
-
-            lax.fori_loop(0, blocks, attend_early, 0)
-    lax.fori_loop(0, blocks, send_block, 0)
-    out_ref[:, group] = send_out[lax.rem(chip, blocks), chip // blocks, core]
+
+        def chunk_step(step, _, chunk=chunk):
+            block_step(step, chunk)
+            return 0
+
+        lax.fori_loop(0, blocks, chunk_step, 0)
+    out_ref[group] = send_out[lax.rem(chip, blocks), chip // blocks, core]
 
     ring_blocks = bias.at[mine, pl.ds(0, chips - 1)]
     pltpu.make_async_copy(ring_blocks, ring_blocks, ring_send_sem).wait()
     pltpu.make_async_copy(whole, whole, pair_send_sem).wait()
     pltpu.make_async_copy(others, others, a2a_send_sem).wait()
-    received = out_ref.at[:, pl.ds(0, 2 * chips - 1)]
+    received = out_ref.at[pl.ds(0, 2 * chips - 1)]
     pltpu.make_async_copy(received, received, out_send_sem).wait()
     pltpu.make_async_copy(received, received, out_recv_sem).wait()
 
@@ -332,7 +324,7 @@
     dma = pltpu.SemaphoreType.DMA
     gathered = pl.pallas_call(
         functools.partial(exchange_kernel, chips, heads),
-        out_shape=jax.ShapeDtypeStruct((local_rows, row_count, width, channels), jnp.bfloat16),
+        out_shape=jax.ShapeDtypeStruct((row_count, width, local_rows, channels), jnp.bfloat16),
         in_specs=[pl.BlockSpec(memory_space=pltpu.HBM)] * 4,
         out_specs=pl.BlockSpec(memory_space=pltpu.VMEM),
         scratch_shapes=[
@@ -349,8 +341,7 @@
             pltpu.VMEM((channels, channels), jnp.float32),
             pltpu.VMEM((width, residues, inner), jnp.bfloat16),
             pltpu.VMEM((width, inner, residues), jnp.bfloat16),
-            pltpu.VMEM((blocks, LANES * width, inner), jnp.float32),
-            pltpu.VMEM((blocks, spread, 2, local_rows, width, inner), jnp.bfloat16),
+            pltpu.VMEM((blocks, spread, 2, width, local_rows, inner), jnp.bfloat16),
             dma((3,)),
             dma,
             dma,
@@ -360,7 +351,7 @@
             dma,
             dma,
             dma,
-            dma((3,)),
+            dma((2,)),
             dma,
             dma,
         ],
@@ -376,8 +367,8 @@
             )
         )
     )
-    gated = gathered.reshape(local_rows, residues, inner)
-    update = jnp.einsum("cnf,fz->cnz", gated, out_weight, preferred_element_type=jnp.float32)
+    gated = gathered.reshape(residues, local_rows, inner)
+    update = jnp.einsum("ncf,fz->cnz", gated, out_weight, preferred_element_type=jnp.float32)
     return (update + out_bias).astype(jnp.bfloat16)
 
 

time: 250 us -> 251 us (level)
  no operation moved by 1% of the time
where the time goes in v3:
time: 251 us
  Pallas kernels  249 us (99%)
    pallas_call x1, Pallas kernels, on_device(): pl.pallas_call(functools.partial(exchange_kernel, chips, heads), out_shap...  249 us

profile of v3, /device:TPU:37, one launch (start us, length us, event | category | flops | bytes accessed | tf_op | source)
XLA Modules:
  0.0 250.8 jit_solution(2251532131290381559)
XLA Ops:
  0.0 0.0 copy-start
  0.0 0.0 copy-start.1
  0.0 249.4 %shard_map.64 = bf16[64,8,8,128]{3,2,1,0:T(8,128)(2,1)S(1)} custom-call(bf16[8,8,2,32,128]{4,3,2,1,0:T(8,128)(2,1)} %bitcast.10, bf16[128,512]{1,0:T(8,128)(2,1)} %proj_hbm.1, f32[1,128]{1,0:T(1,128)} %bitcast.12, bf16[4,128]{1,0:T(4,128)(2,1)} %bitcast.11), custom_call_target="tpu_custom_call" | custom-call | tf_op jit(solution)/shard_map/pallas_call | solution.py:325
  249.4 0.0 copy-done
  249.4 0.0 copy-done.1
  249.4 1.4 fusion
Async XLA Ops:
  0.0 249.4 %copy-start = (bf16[128,128]{1,0:T(8,128)(2,1)S(1)}, bf16[128,128]{1,0:T(8,128)(2,1)}, u32[]{:S(2)}) copy-start(bf16[128,128]{1,0:T(8,128)(2,1)} %param.10) | copy-start | bytes 98308
  0.0 249.4 %copy-start.1 = (f32[128]{0:T(128)S(1)}, f32[128]{0:T(128)}, u32[]{:S(2)}) copy-start(f32[128]{0:T(128)} %param.11) | copy-start | bytes 1540

commit v4 on v3

--- a/solution.py
+++ b/solution.py
@@ -64,7 +64,7 @@
     core = lax.rem(row, 2)
     partner = row + 1 - 2 * core
     last = chips // 2
-    first = width // 2
+    first = 3 * width // 4
     chunks = ((0, first), (first, width - first))
 
     def at(distance):
@@ -83,14 +83,6 @@
     ]
     for copy in weight_copies:
         copy.start()
-    for copy in weight_copies:
-        copy.wait()
-
-    proj_t[...] = proj_ref[...].astype(jnp.float32).T.astype(jnp.bfloat16)
-    gate_col[...] = jnp.broadcast_to(gate_bias_ref[...], (channels, channels)).T
-    bias_w = bias_weight_ref[...].astype(jnp.float32)
-    bias_w = jnp.concatenate([bias_w, jnp.zeros((8 - heads, channels), jnp.float32)], axis=0).astype(jnp.bfloat16)
-
     pl.semaphore_wait(barrier, 3)
     swap = pltpu.make_async_remote_copy(
         src_ref=x_ref.at[:, :, 1 - core],
@@ -101,6 +93,14 @@
         device_id_type=MESH,
     )
     swap.start()
+    for copy in weight_copies:
+        copy.wait()
+
+    proj_t[...] = proj_ref[...].astype(jnp.float32).T.astype(jnp.bfloat16)
+    gate_col[...] = jnp.broadcast_to(gate_bias_ref[...], (channels, channels)).T
+    bias_w = bias_weight_ref[...].astype(jnp.float32)
+    bias_w = jnp.concatenate([bias_w, jnp.zeros((8 - heads, channels), jnp.float32)], axis=0).astype(jnp.bfloat16)
+
     keep.wait()
 
     def normalize_row(part, line):
@@ -181,6 +181,8 @@
         return 0
 
     lax.fori_loop(0, chips, round_chunk, 0)
+    column_copy(1, 0).start()
+    column_copy(-1, 0).start()
     cols[:, chip // blocks, lax.rem(chip, blocks)] = send_buf[chip]
 
     def chip_at(distance):
@@ -198,15 +200,18 @@
 
         pair_copy(behind).start()
         pair_copy(ahead).start()
-        column_copy(step, 0).start()
-        column_copy(-step, 0).start()
+        column_copy(step + 1, 0).start()
+
+        @pl.when(step + 1 < last)
+        def _():
+            column_copy(-step - 1, 0).start()
+
         return 0
 
     lax.fori_loop(1, last, ring_step, 0)
     opposite = chip_at(-last)
     ring_copy(opposite, last - 1, 0, at(1)).wait_recv()
     pair_copy(opposite).start()
-    column_copy(last, 0).start()
     for chunk in range(1, len(chunks)):
         column_copy(last, chunk).start()
 
@@ -255,11 +260,10 @@
         rows = gated_t.T.reshape(spread, 2, local_rows, channels)
         send_out[block, :, :, column] = rows.astype(jnp.bfloat16)
 
-    def out_copy(block, a, target_core, chunk):
-        part = pl.ds(*chunks[chunk])
+    def out_copy(block, a, target_core):
         return pltpu.make_async_remote_copy(
-            src_ref=send_out.at[block, a, target_core, part],
-            dst_ref=out_ref.at[group, part],
+            src_ref=send_out.at[block, a, target_core],
+            dst_ref=out_ref.at[group],
             send_sem=out_send_sem,
             recv_sem=out_recv_sem,
             device_id={"row": 2 * (a * blocks + block) + target_core},
@@ -275,6 +279,8 @@
             return 0
 
         lax.fori_loop(start, start + count, column_step, 0)
+        if chunk < len(chunks) - 1:
+            return
 
         def send(index, _):
             order = index // 2
@@ -284,7 +290,7 @@
 
             @pl.when(2 * target_chip + target_core != row)
             def _():
-                out_copy(block, target_chip // blocks, target_core, chunk).start()
+                out_copy(block, target_chip // blocks, target_core).start()
 
             return 0
 

time: 251 us -> 257 us (1.024)
  Pallas kernels: 249 us -> 255 us
    pallas_call x1, Pallas kernels: 249 us -> 255 us  [on_device(): pl.pallas_call(functools.partial(exchange_kernel, chips, heads), out_shap...]
where the time goes in v4:
time: 257 us; the launch traced here: 256 us
  Pallas kernels  255 us (99%)
    pallas_call x1, Pallas kernels, on_device(): pl.pallas_call(functools.partial(exchange_kernel, chips, heads), out_shap...  255 us

profile of v4, /device:TPU:37, one launch (start us, length us, event | category | flops | bytes accessed | tf_op | source)
XLA Modules:
  0.0 256.4 jit_solution(6632959693257727183)
XLA Ops:
  0.0 0.0 copy-start
  0.0 0.0 copy-start.1
  0.0 255.0 %shard_map.64 = bf16[64,8,8,128]{3,2,1,0:T(8,128)(2,1)S(1)} custom-call(bf16[8,8,2,32,128]{4,3,2,1,0:T(8,128)(2,1)} %bitcast.10, bf16[128,512]{1,0:T(8,128)(2,1)} %proj_hbm.1, f32[1,128]{1,0:T(1,128)} %bitcast.12, bf16[4,128]{1,0:T(4,128)(2,1)} %bitcast.11), custom_call_target="tpu_custom_call" | custom-call | tf_op jit(solution)/shard_map/pallas_call | solution.py:331
  255.0 0.0 copy-done
  255.0 0.0 copy-done.1
  255.0 1.4 fusion
Async XLA Ops:
  0.0 255.0 %copy-start = (bf16[128,128]{1,0:T(8,128)(2,1)S(1)}, bf16[128,128]{1,0:T(8,128)(2,1)}, u32[]{:S(2)}) copy-start(bf16[128,128]{1,0:T(8,128)(2,1)} %param.10) | copy-start | bytes 98308
  0.0 255.0 %copy-start.1 = (f32[128]{0:T(128)S(1)}, f32[128]{0:T(128)}, u32[]{:S(2)}) copy-start(f32[128]{0:T(128)} %param.11) | copy-start | bytes 1540

commit v5 on v2

--- a/solution.py
+++ b/solution.py
@@ -84,14 +84,6 @@
     ]
     for copy in weight_copies:
         copy.start()
-    for copy in weight_copies:
-        copy.wait()
-
-    proj_t[...] = proj_ref[...].astype(jnp.float32).T.astype(jnp.bfloat16)
-    gate_col[...] = jnp.broadcast_to(gate_bias_ref[...], (channels, channels)).T
-    bias_w = bias_weight_ref[...].astype(jnp.float32)
-    bias_w = jnp.concatenate([bias_w, jnp.zeros((8 - heads, channels), jnp.float32)], axis=0).astype(jnp.bfloat16)
-
     pl.semaphore_wait(barrier, 3)
     swap = pltpu.make_async_remote_copy(
         src_ref=x_ref.at[:, :, 1 - core],
@@ -102,6 +94,14 @@
         device_id_type=MESH,
     )
     swap.start()
+    for copy in weight_copies:
+        copy.wait()
+
+    proj_t[...] = proj_ref[...].astype(jnp.float32).T.astype(jnp.bfloat16)
+    gate_col[...] = jnp.broadcast_to(gate_bias_ref[...], (channels, channels)).T
+    bias_w = bias_weight_ref[...].astype(jnp.float32)
+    bias_w = jnp.concatenate([bias_w, jnp.zeros((8 - heads, channels), jnp.float32)], axis=0).astype(jnp.bfloat16)
+
     keep.wait()
 
     def normalize_row(part, line):

time: 250 us -> 250 us (level)
  no operation moved by 1% of the time
where the time goes in v5:
time: 250 us; the launch traced here: 248 us
  Pallas kernels  246 us (98%)
    pallas_call x1, Pallas kernels, on_device(): pl.pallas_call(functools.partial(exchange_kernel, chips, heads), out_shap...  246 us

profile of v5, /device:TPU:37, one launch (start us, length us, event | category | flops | bytes accessed | tf_op | source)
XLA Modules:
  0.0 247.9 jit_solution(8163893542569912105)
XLA Ops:
  0.0 0.0 copy-start
  0.0 0.0 copy-start.1
  0.0 246.5 %shard_map.64 = bf16[8,64,8,128]{3,2,1,0:T(8,128)(2,1)S(1)} custom-call(bf16[8,8,2,32,128]{4,3,2,1,0:T(8,128)(2,1)} %bitcast.9, bf16[128,512]{1,0:T(8,128)(2,1)} %proj_hbm.1, f32[1,128]{1,0:T(1,128)} %bitcast.11, bf16[4,128]{1,0:T(4,128)(2,1)} %bitcast.10), custom_call_target="tpu_custom_call" | custom-call | tf_op jit(solution)/shard_map/pallas_call | solution.py:333
  246.5 0.0 copy-done
  246.5 0.0 copy-done.1
  246.5 1.4 add_convert_fusion
Async XLA Ops:
  0.0 246.5 %copy-start = (bf16[128,128]{1,0:T(8,128)(2,1)S(1)}, bf16[128,128]{1,0:T(8,128)(2,1)}, u32[]{:S(2)}) copy-start(bf16[128,128]{1,0:T(8,128)(2,1)} %param.10) | copy-start | bytes 98308
  0.0 246.5 %copy-start.1 = (f32[128]{0:T(128)S(1)}, f32[128]{0:T(128)}, u32[]{:S(2)}) copy-start(f32[128]{0:T(128)} %param.11) | copy-start | bytes 1540
